TPU v7x, 32 devices: a 4x4x1 block of a 4x4x8 slice. The times are simulated.
32 devices in a mesh: dp: 2 (over z, core), tp: 16 (over x, y).
Axes of the slice: x: 4, y: 4, z: 1, core: 2. Of those that a mesh axis runs over, the one named last changes fastest.
The devices are a block of a 4x4x8 slice.
Arguments:
- x: bfloat16 [4096, 2048], P('dp'), parts along dimension 0
- dy: bfloat16 [4096, 2048], P('dp'), parts along dimension 0
- gate: bfloat16 [4096, 8192], P('dp', 'tp'), parts along dimension 0
- up: bfloat16 [4096, 8192], P('dp', 'tp'), parts along dimension 0
- w_gate: bfloat16 [2048, 8192], P(None, 'tp')
- w_up: bfloat16 [2048, 8192], P(None, 'tp')
- w_down: bfloat16 [8192, 2048], P('tp')
Outputs:
- output 1: bfloat16 [4096, 2048], P('dp'), parts along dimension 0
- output 2: bfloat16 [4096, 8192], P('dp', 'tp'), parts along dimension 0
- output 3: bfloat16 [4096, 8192], P('dp', 'tp'), parts along dimension 0
- output 4: bfloat16 [16384, 2048], P(('dp', 'tp')), parts along dimension 0
There are 2 independent parts. A program takes and returns all parts, laid end to end along the dimension named above; an argument that names none is the same for every part.
All inputs are finite; a program needn't handle non-finite values.
Results may differ from a plain program's by a relative error of at most 0.012.
Values are sent between devices in bfloat16 or wider.
A program may use at most 768 MiB of HBM per device.

v0:
```python
import jax
import jax.numpy as jnp
from jax import lax
from jax.sharding import PartitionSpec as P


def act(gate, up):
    return jax.nn.silu(gate) * up


def solution(mesh):
    def step(x, dy, gate, up, w_gate, w_up, w_down):
        hidden, back = jax.vjp(act, gate.astype(jnp.float32), up.astype(jnp.float32))
        d_hidden = jnp.dot(dy, w_down.T, preferred_element_type=jnp.float32)
        d_gate, d_up = (g.astype(jnp.bfloat16) for g in back(d_hidden))
        term = jnp.dot(d_gate, w_gate.T, preferred_element_type=jnp.float32) + jnp.dot(d_up, w_up.T, preferred_element_type=jnp.float32)
        dx = lax.psum(term.astype(jnp.bfloat16), "tp")
        dw_gate = jnp.dot(x.T, d_gate, preferred_element_type=jnp.float32)
        dw_up = jnp.dot(x.T, d_up, preferred_element_type=jnp.float32)
        dw_down = jnp.dot(hidden.astype(jnp.bfloat16).T, dy, preferred_element_type=jnp.float32)
        return dx, *(g.astype(jnp.bfloat16) for g in (dw_gate, dw_up, dw_down))

    tokens, columns, rows = P("dp", None), P(None, "tp"), P("tp", None)
    return jax.shard_map(
        step,
        mesh=mesh,
        in_specs=(tokens, tokens, P("dp", "tp"), P("dp", "tp"), columns, columns, rows),
        out_specs=(tokens, P("dp", "tp"), P("dp", "tp"), P(("dp", "tp"), None)),
        check_vma=False,
    )
```

profile of v0, /device:TPU:97, one launch (start us, length us, event | category | flops | bytes accessed | tf_op | source)
XLA Modules:
  0.0 195.1 jit_solution(2480916002338006650)
XLA Ops:
  7.2 0.0 copy-start
  7.2 0.1 all-reduce.2.cloned.1.call-start
  7.3 13.3 %fusion.6 = (bf16[2048,512]{1,0:T(8,128)(2,1)S(1)}, f32[2048,512]{1,0:T(8,128)}) fusion(bf16[2048,512]{1,0:T(8,128)(2,1)} %param.9, bf16[2048,512]{1,0:T(8,128)(2,1)} %param.10, bf16[2048,2048]{1,0:T(8,128)(2,1)} %param.8, bf16[512,2048]{1,0:T(8,128)(2,1)} %param.13), kind=kOutput, calls=%fused_computation.13 | convolution fusion | flops 4308598784 | bytes 20971520 | tf_op jit(solution)/shard_map/dot_general | solution.py:14
  20.6 0.0 copy-start.2
  20.6 0.0 copy-done
  20.6 8.3 %fusion.11 = f32[2048,2048]{1,0:T(8,128)} fusion(bf16[2048,512]{1,0:T(8,128)(2,1)S(1)} %get-tuple-element.8, bf16[2048,512]{1,0:T(8,128)(2,1)S(1)} %copy-done), kind=kOutput, calls=%fused_computation.21 | convolution fusion | flops 4294967296 | bytes 20971520 | tf_op jit(solution)/shard_map/dot_general | solution.py:16
  28.9 0.0 copy-done.2
  28.9 16.5 %add_convert_fusion = bf16[2048,2048]{1,0:T(8,128)(2,1)} fusion(f32[2048,2048]{1,0:T(8,128)} %fusion.11, bf16[2048,512]{1,0:T(8,128)(2,1)} %param.12, f32[2048,512]{1,0:T(8,128)} %get-tuple-element.9, bf16[2048,512]{1,0:T(8,128)(2,1)} %param.9), kind=kOutput, calls=%fused_computation | convolution fusion | flops 4310695936 | bytes 33554432 | tf_op jit(solution)/shard_map/dot_general | solution.py:16
  45.4 0.1 all-reduce.2.cloned.1.call-update
  45.5 8.6 %fusion.7 = bf16[2048,512]{0,1:T(8,128)(2,1)S(1)} fusion(bf16[2048,512]{1,0:T(8,128)(2,1)} %copy-done.2, bf16[2048,2048]{1,0:T(8,128)(2,1)} %param.7), kind=kOutput, calls=%fused_computation.18 | convolution fusion | flops 4296015872 | bytes 12582912 | tf_op jit(solution)/shard_map/dot_general | solution.py:18
  54.1 2.5 %copy.11 = bf16[2048,512]{1,0:T(8,128)(2,1)} copy(bf16[2048,512]{0,1:T(8,128)(2,1)S(1)} %fusion.7) | data formatting | bytes 4194304
  56.6 10.1 %fusion.8 = bf16[2048,512]{0,1:T(8,128)(2,1)S(1)} fusion(bf16[2048,2048]{1,0:T(8,128)(2,1)} %param.7, f32[2048,512]{1,0:T(8,128)} %get-tuple-element.9, bf16[2048,512]{1,0:T(8,128)(2,1)} %param.9), kind=kOutput, calls=%fused_computation.19 | convolution fusion | flops 4303355904 | bytes 16777216 | tf_op jit(solution)/shard_map/dot_general | solution.py:19
  66.7 2.5 %copy.12 = bf16[2048,512]{1,0:T(8,128)(2,1)} copy(bf16[2048,512]{0,1:T(8,128)(2,1)S(1)} %fusion.8) | data formatting | bytes 4194304
  69.2 11.1 %convolution_convert_fusion = bf16[512,2048]{1,0:T(8,128)(2,1)} fusion(bf16[2048,2048]{1,0:T(8,128)(2,1)} %param.8, bf16[2048,512]{1,0:T(8,128)(2,1)} %param.10, bf16[2048,512]{1,0:T(8,128)(2,1)} %param.9), kind=kOutput, calls=%fused_computation.15 | convolution fusion | flops 4304404480 | bytes 14680064 | tf_op jit(solution)/shard_map/dot_general | solution.py:20
  80.3 99.4 %all-reduce.2.cloned.1.call-done = bf16[2048,2048]{1,0:T(8,128)(2,1)} async-done(((bf16[2048,2048]{1,0:T(8,128)(2,1)}), bf16[2048,2048]{1,0:T(8,128)(2,1)}) %all-reduce.2.cloned.1.call-update) | async-done | bytes 8388624 | tf_op jit(solution)/shard_map/psum | solution.py:17
  179.7 0.0 copy-start.1
  179.7 8.6 %copy.14 = bf16[2048,2048]{1,0:T(8,128)(2,1)} copy(bf16[2048,2048]{1,0:T(8,128)(2,1)} %all-reduce.2.cloned.1.call-done) | data formatting | bytes 16777216
  188.3 0.0 copy-done.1
Async XLA Ops:
  7.2 13.4 %copy-start = (bf16[2048,512]{1,0:T(8,128)(2,1)S(1)}, bf16[2048,512]{1,0:T(8,128)(2,1)}, u32[]{:S(2)}) copy-start(bf16[2048,512]{1,0:T(8,128)(2,1)} %param.11) | copy-start | bytes 6291460
  7.2 172.5 %all-reduce.2.cloned.1.call-start = ((), (), s32[]{:S(2)}) async-start(), calls=%async_computation | async-start | bytes 16777216 | tf_op jit(solution)/shard_map/psum | solution.py:17
  20.6 8.3 %copy-start.2 = (bf16[2048,512]{1,0:T(8,128)(2,1)}, bf16[2048,512]{1,0:T(8,128)(2,1)S(1)}, u32[]{:S(2)}) copy-start(bf16[2048,512]{1,0:T(8,128)(2,1)S(1)} %get-tuple-element.8) | copy-start | bytes 6291460
  179.7 8.6 %copy-start.1 = (bf16[2048,512]{1,0:T(8,128)(2,1)S(1)}, bf16[2048,512]{1,0:T(8,128)(2,1)}, u32[]{:S(2)}) copy-start(bf16[2048,512]{1,0:T(8,128)(2,1)} %param.11) | copy-start | bytes 6291460
Sparse Core Ops, SparseCore 0:
  45.6 134.0 all-reduce.1
where the time goes:
time: 195 us
  waiting for transfers between devices  99.4 us (51%)
  matrix products  67.9 us (35%)
  between operations  14.1 us (7%)
  local copies, waits for them, and re-layouts  13.6 us (7%)
    psum x1, waiting for transfers between devices, step(): dx = lax.psum(term.astype(jnp.bfloat16), 'tp')  99.4 us
    dot_general x1, matrix products, step(): jnp.dot(d_up, w_up.T, preferred_element_type=jnp.float32)  16.5 us
    unnamed x9, local copies, waits for them, and re-layouts  13.6 us
    dot_general x1, matrix products, step(): d_hidden = jnp.dot(dy, w_down.T, preferred_element_type=jnp.float32)  13.3 us
    dot_general x1, matrix products, step(): jnp.dot(hidden.astype(jnp.bfloat16).T, dy, preferred_element_type=jnp.flo...  11.1 us
    dot_general x1, matrix products, step(): dw_up = jnp.dot(x.T, d_up, preferred_element_type=jnp.float32)  10.1 us
    dot_general x1, matrix products, step(): dw_gate = jnp.dot(x.T, d_gate, preferred_element_type=jnp.float32)  8.59 us
    dot_general x1, matrix products, step(): jnp.dot(d_gate, w_gate.T, preferred_element_type=jnp.float32)  8.33 us
  transfers between devices with their start and end apart: 1, of which 1 were waited for; matrix products, arithmetic and copies ran while one was open for 18% of the time, Pallas kernels for 0%

commit v1 on v0

v1 whole, which is shorter than its diff:
```python
import functools
import math

import jax
import jax.numpy as jnp
from jax import lax
from jax.experimental import pallas as pl
from jax.experimental.pallas import tpu as pltpu
from jax.sharding import PartitionSpec as P

SIDE = 4
CHUNKS = 4
A, B, C, A2, B2, C2, G20, G21, R2, G10, G11, R1 = range(12)
NT = (((1,), (1,)), ((), ()))
NN = (((1,), (0,)), ((), ()))


def dot(a, b, dims):
    return lax.dot_general(a, b, dims, preferred_element_type=jnp.float32)


def chunk_rows(rows):
    return [rows // CHUNKS] * CHUNKS


def body(chunks, x, dy, gate, up, w_gate, w_up, w_down, dx, dw_gate, dw_up, dw_down,
         wd, wgu, dgu, hid_t, dyb, gb, ub, xb, xt, st_a, st_b, r_a, r_b, r_c, c_term, own,
         s2_a, s2_b, r2_a, r2_b, r2_c, lsem, ssem, rsem):
    d = x.shape[1]
    ff = gate.shape[1]
    nb = d // (2 * SIDE)
    starts = [sum(chunks[:k]) for k in range(len(chunks))]
    t = lax.axis_index("tp")
    px, py = lax.div(t, SIDE), lax.rem(t, SIDE)

    def to(axis, s):
        step = 1 + (SIDE - 2) * s
        return lax.rem(px + (1 - axis) * step, SIDE) * SIDE + lax.rem(py + axis * step, SIDE)

    def on(axis):
        return px * (1 - axis) + py * axis

    def local(src, dst, i):
        return pltpu.make_async_copy(src, dst, lsem.at[i])

    def send(kind, k, i, src, dst, axis):
        s = lax.rem(i, 2)
        return pltpu.make_async_remote_copy(
            src_ref=src, dst_ref=dst, send_sem=ssem.at[kind, k, i], recv_sem=rsem.at[kind, k, i],
            device_id={"tp": to(axis, s)}, device_id_type=pl.DeviceIdType.MESH,
        )

    def loop(n, f):
        lax.fori_loop(0, n, lambda i, c: (f(i), c)[1], 0)

    nk = len(chunks)
    load_wd = local(w_down, wd, 0)
    load_wg = local(w_gate, wgu.at[:, pl.ds(0, ff)], 1)
    load_wu = local(w_up, wgu.at[:, pl.ds(ff, ff)], 2)

    def load_dy(k):
        rows = pl.ds(starts[k], chunks[k])
        return local(dy.at[rows], dyb.at[rows], 3 + k)

    def load_gu(k):
        rows, slot = pl.ds(starts[k], chunks[k]), pl.ds(0, chunks[k])
        return (local(gate.at[rows], gb.at[k % 2, slot], 3 + nk + k),
                local(up.at[rows], ub.at[k % 2, slot], 3 + 2 * nk + k))

    def load_x(j, slot):
        return local(x.at[:, pl.ds(pl.multiple_of(j * nb, nb), nb)], xb.at[slot], 3 + 3 * nk + slot)

    load_wd.start()
    load_dy(0).start()
    for c in load_gu(0):
        c.start()
    load_wg.start()
    load_wu.start()
    if nk > 1:
        load_dy(1).start()
        for c in load_gu(1):
            c.start()
    for k in range(2, nk):
        load_dy(k).start()
    load_x(0, 0).start()
    load_x(1, 1).start()

    barrier = pltpu.get_barrier_semaphore()
    for axis in range(2):
        for s in range(2):
            pl.semaphore_signal(barrier, inc=1, device_id={"tp": to(axis, s)}, device_id_type=pl.DeviceIdType.MESH)

    def ru(k):
        return chunks[k] // 2

    def rs(k):
        return chunks[k] // (2 * SIDE)

    def unit_rows(k, u):
        return pl.ds(starts[k] + u * ru(k), ru(k))

    def u1(k):
        return pl.ds(starts[k] // 2, ru(k))

    def u2(k):
        return pl.ds(starts[k] // (2 * SIDE), rs(k))

    def term(k, u, h, j):
        w = pl.ds(pl.multiple_of((h * SIDE + j) * nb, nb), nb)
        return dot(dgu[unit_rows(k, u), :], wgu[w, :], NT)

    def sub(k, q):
        return pl.ds(pl.multiple_of(starts[k] // 2 + q * rs(k), 16), rs(k))

    def region(k, u, h, j, q=None):
        cols = pl.ds(pl.multiple_of((h * SIDE + j) * nb, nb), nb)
        if q is None:
            return dx.at[pl.ds(pl.multiple_of(starts[k] + u * ru(k), 16), ru(k)), cols]
        return dx.at[pl.ds(pl.multiple_of(starts[k] + u * ru(k) + q * rs(k), 16), rs(k)), cols]

    def mod(v):
        return lax.rem(v, SIDE)

    def m_a(k, i, h):
        return send(A, k, i, st_a.at[i, u1(k)], r_a.at[i, u1(k)], h)

    def m_b(k, i, h):
        return send(B, k, i, st_b.at[i, u1(k)], r_b.at[i, u1(k)], h)

    def m_c(k, i, h):
        return send(C, k, i, r_a.at[i, u1(k)], r_c.at[i, u1(k)], h)

    def m_a2(k, i, h):
        return send(A2, k, i, s2_a.at[i, u2(k)], r2_a.at[i, u2(k)], 1 - h)

    def m_b2(k, i, h):
        return send(B2, k, i, s2_b.at[i, u2(k)], r2_b.at[i, u2(k)], 1 - h)

    def m_c2(k, i, h):
        return send(C2, k, i, r2_a.at[i, u2(k)], r2_c.at[i, u2(k)], 1 - h)

    def m_g2(k, i, h, s, n):
        u = s if n == 0 else 1 - s
        where = region(k, u, h, on(h), on(1 - h))
        return send(G20 + n, k, i, where, where, 1 - h)

    def m_r2(k, i, h, s):
        where = region(k, s, h, on(h), mod(on(1 - h) + SIDE - 1 + 2 * s))
        return send(R2, k, i, where, where, 1 - h)

    def m_g1(k, i, h, s, n):
        u = s if n == 0 else 1 - s
        where = region(k, u, h, on(h))
        return send(G10 + n, k, i, where, where, h)

    def m_r1(k, i, h, s):
        where = region(k, s, h, mod(on(h) + SIDE - 1 + 2 * s))
        return send(R1, k, i, where, where, h)

    def hs(i):
        return lax.div(i, 2), lax.rem(i, 2)

    def bf(v):
        return v.astype(jnp.bfloat16)

    def f32(v):
        return v.astype(jnp.float32)

    def stage_hidden(k):
        sm = min(256, chunks[k])
        nn = min(256, ff)
        load_dy(k).wait()
        for c in load_gu(k):
            c.wait()
        if k == 0:
            load_wd.wait()

        def tile(m):
            rows = pl.ds(pl.multiple_of(starts[k] + m * sm, sm), sm)
            part = pl.ds(pl.multiple_of(m * sm, sm), sm)
            for n in range(ff // nn):
                cols = pl.ds(n * nn, nn)
                dh = dot(dyb[rows, :], wd[cols, :], NT)
                g, v = f32(gb[k % 2, part, cols]), f32(ub[k % 2, part, cols])
                sg = 1.0 / (1.0 + jnp.exp(-g))
                silu = g * sg
                dgu[rows, cols] = bf(dh * v * (sg + silu * (1.0 - sg)))
                dgu[rows, pl.ds(ff + n * nn, nn)] = bf(dh * silu)
                hid_t[cols, rows] = bf(silu * v).T

        loop(chunks[k] // sm, tile)
        if k + 2 < nk:
            for c in load_gu(k + 2):
                c.start()

    def stage_a(k):
        if k == 0:
            load_wg.wait()
            load_wu.wait()

        def half(h):
            for s in range(2):
                st_a[2 * h + s, u1(k), :] = bf(term(k, s, h, mod(on(h) + 2)))
            if k == 0:
                pl.when(h == 0)(lambda: pl.semaphore_wait(barrier, 4))
            for s in range(2):
                m_a(k, 2 * h + s, h).start()

        loop(2, half)

    def stage_b(k):
        def each(i):
            h, s = hs(i)
            j = mod(on(h) + 1 + 2 * s)
            st_b[i, u1(k), :] = bf(term(k, 1 - s, h, j))
            m_b(k, i, h).start()
            c_term[i, u1(k), :] = term(k, s, h, j)

        loop(4, each)

    def stage_c(k):
        def each(i):
            h, s = hs(i)
            m_a(k, i, h).wait_recv()
            r_a[i, u1(k), :] = bf(c_term[i, u1(k), :] + f32(r_a[i, u1(k), :]))
            m_c(k, i, h).start()

        loop(4, each)

    def stage_own(k):
        def each(h):
            for u in range(2):
                own[h, u, u1(k), :] = term(k, u, h, on(h))

        loop(2, each)

    def stage_o(k):
        def each(h):
            for i in range(2):
                m_b(k, 2 * h + i, h).wait_recv()
                m_c(k, 2 * h + i, h).wait_recv()
            for u in range(2):
                own[h, u, u1(k), :] += f32(r_c[2 * h + u, u1(k), :]) + f32(r_b[2 * h + 1 - u, u1(k), :])
            q = on(1 - h)
            for s in range(2):
                s2_a[2 * h + s, u2(k), :] = bf(own[h, s, sub(k, mod(q + 2)), :])
                m_a2(k, 2 * h + s, h).start()
            for s in range(2):
                s2_b[2 * h + s, u2(k), :] = bf(own[h, 1 - s, sub(k, mod(q + 1 + 2 * s)), :])
                m_b2(k, 2 * h + s, h).start()

        loop(2, each)

    def stage_c2(k):
        def each(i):
            h, s = hs(i)
            m_a2(k, i, h).wait_recv()
            r2_a[i, u2(k), :] = bf(own[h, s, sub(k, mod(on(1 - h) + 1 + 2 * s)), :] + f32(r2_a[i, u2(k), :]))
            m_c2(k, i, h).start()

        loop(4, each)

    def stage_o2(k):
        def each(h):
            for i in range(2):
                m_b2(k, 2 * h + i, h).wait_recv()
                m_c2(k, 2 * h + i, h).wait_recv()
            q = on(1 - h)
            for u in range(2):
                total = own[h, u, sub(k, q), :] + f32(r2_c[2 * h + u, u2(k), :]) + f32(r2_b[2 * h + 1 - u, u2(k), :])
                region(k, u, h, on(h), q)[...] = bf(total)
            for n in range(2):
                for s in range(2):
                    m_g2(k, 2 * h + s, h, s, n).start()

        loop(2, each)

    def stage_r2(k):
        def each(h):
            for s in range(2):
                m_g2(k, 2 * h + s, h, s, 0).wait_recv()
                m_r2(k, 2 * h + s, h, s).start()

        loop(2, each)

    def stage_g1(k):
        def each(h):
            for s in range(2):
                m_g2(k, 2 * h + s, h, s, 1).wait_recv()
                m_r2(k, 2 * h + s, h, s).wait_recv()
            for n in range(2):
                for s in range(2):
                    m_g1(k, 2 * h + s, h, s, n).start()

        loop(2, each)

    def stage_r1(k):
        def each(h):
            for s in range(2):
                m_g1(k, 2 * h + s, h, s, 0).wait_recv()
                m_r1(k, 2 * h + s, h, s).start()

        loop(2, each)

    def stage_end(k):
        def each(h):
            for s in range(2):
                i = 2 * h + s
                m_g1(k, i, h, s, 1).wait_recv()
                m_r1(k, i, h, s).wait_recv()

        loop(2, each)

    def sent(k):
        def each(h):
            for s in range(2):
                i = 2 * h + s
                for m in (m_a, m_b, m_c, m_a2, m_b2, m_c2):
                    m(k, i, h).wait_send()
                for n in range(2):
                    m_g2(k, i, h, s, n).wait_send()
                    m_g1(k, i, h, s, n).wait_send()
                m_r2(k, i, h, s).wait_send()
                m_r1(k, i, h, s).wait_send()

        loop(2, each)

    tiles = d // nb

    def tile_gu(j):
        slot = lax.rem(j, 2)
        load_x(j, slot).wait()
        xt[...] = xb[slot].T
        pl.when(j + 2 < tiles)(lambda: load_x(j + 2, slot).start())
        nn = min(256, ff)
        rows = pl.ds(pl.multiple_of(j * nb, nb), nb)

        def cols_of(n):
            cols = pl.ds(pl.multiple_of(n * nn, nn), nn)
            dw_gate[rows, cols] = bf(dot(xt[...], dgu[:, cols], NN))
            up_cols = pl.ds(pl.multiple_of(ff + n * nn, nn), nn)
            dw_up[rows, cols] = bf(dot(xt[...], dgu[:, up_cols], NN))

        loop(ff // nn, cols_of)

    def tile_d(j):
        cols = pl.ds(pl.multiple_of(j * nb, nb), nb)
        mm = min(256, ff)

        def rows_of(m):
            rows = pl.ds(pl.multiple_of(m * mm, mm), mm)
            dw_down[rows, cols] = bf(dot(hid_t[rows, :], dyb[:, cols], NN))

        loop(ff // mm, rows_of)

    done = [0]

    def weights(n):
        lo, hi = done[0], min(done[0] + n, 2 * tiles)
        done[0] = hi
        a, b = min(lo, tiles), min(hi, tiles)
        if b > a:
            lax.fori_loop(a, b, lambda j, c: (tile_gu(j), c)[1], 0)
        a, b = max(lo, tiles) - tiles, max(hi, tiles) - tiles
        if b > a:
            lax.fori_loop(a, b, lambda j, c: (tile_d(j), c)[1], 0)

    for name, k in order():
        if name == "w":
            weights(k)
        else:
            {"h": stage_hidden, "a": stage_a, "b": stage_b, "c": stage_c, "own": stage_own, "o": stage_o, "c2": stage_c2,
             "o2": stage_o2, "r2": stage_r2, "g1": stage_g1, "r1": stage_r1, "end": stage_end}[name](k)
    weights(2 * tiles)
    for k in range(nk):
        sent(k)


ORDER = (
    "h0 a0 b0", "h1 a1 b1", "c0 own0", "h2 a2 b2", "c1 o0 own1", "h3 a3 b3", "c20 c2 own2 o1", "w1 o20 c21 own3", "w1 c3 r20 o2",
    "w1 o21 c22", "w1 g10 r21 o3", "w1 o22", "w1 g11 c23", "w1 r22", "w1 r10 o23", "w1 g12", "w1 r11 r23", "w2 r12 g13", "w3 r13",
    "w4 end0 end1", "end2 end3",
)


def order():
    return [(word[:-1], int(word[-1])) for words in ORDER for word in words.split()]


def write_out(*refs):
    n = (len(refs) - 1) // 2
    sem = refs[-1]
    copies = []
    for a, o in zip(refs[:n], refs[n : 2 * n]):
        parts = 4 if a.shape[0] * a.shape[1] > 2**21 else 1
        size = a.shape[0] // parts
        for i in range(parts):
            rows = pl.ds(i * size, size)
            copies.append(pltpu.make_async_copy(a.at[rows], o.at[rows], sem.at[len(copies)]))
    for c in copies:
        c.start()
    for c in copies:
        c.wait()


def solution(mesh):
    assert mesh.shape["tp"] == SIDE * SIDE

    def step(x, dy, gate, up, w_gate, w_up, w_down):
        rows, d = x.shape
        ff = gate.shape[1]
        nb = d // (2 * SIDE)
        chunks = chunk_rows(rows)
        nk = len(chunks)
        most = max(chunks)
        bf16, f32 = jnp.bfloat16, jnp.float32
        any_space = pl.BlockSpec(memory_space=pl.ANY)
        vmem = pl.BlockSpec(memory_space=pltpu.VMEM)
        shapes = [(rows, d), (d, ff), (d, ff), (ff, d)]
        flops = 2 * 6 * rows * d * ff
        results = pl.pallas_call(
            functools.partial(body, chunks),
            out_shape=[pltpu.VMEM(s, bf16) for s in shapes],
            in_specs=[any_space] * 7,
            out_specs=[vmem] * 4,
            scratch_shapes=[
                pltpu.VMEM((ff, d), bf16),
                pltpu.VMEM((d, 2 * ff), bf16),
                pltpu.VMEM((rows, 2 * ff), bf16),
                pltpu.VMEM((ff, rows), bf16),
                pltpu.VMEM((rows, d), bf16),
                pltpu.VMEM((2, most, ff), bf16),
                pltpu.VMEM((2, most, ff), bf16),
                pltpu.VMEM((2, rows, nb), bf16),
                pltpu.VMEM((nb, rows), bf16),
                *[pltpu.VMEM((4, rows // 2, nb), bf16) for _ in range(5)],
                pltpu.VMEM((4, rows // 2, nb), f32),
                pltpu.VMEM((2, 2, rows // 2, nb), f32),
                *[pltpu.VMEM((4, rows // (2 * SIDE), nb), bf16) for _ in range(5)],
                pltpu.SemaphoreType.DMA((5 + 3 * nk,)),
                pltpu.SemaphoreType.DMA((12, nk, 4)),
                pltpu.SemaphoreType.DMA((12, nk, 4)),
            ],
            compiler_params=pltpu.CompilerParams(
                collective_id=0, has_side_effects=True, vmem_limit_bytes=48 * 2**20
            ),
            cost_estimate=pl.CostEstimate(flops=flops, bytes_accessed=30 * 2**20, transcendentals=rows * ff),
            name="backward",
        )(x, dy, gate, up, w_gate, w_up, w_down)
        return pl.pallas_call(
            write_out,
            out_shape=[jax.ShapeDtypeStruct(s, bf16) for s in shapes],
            in_specs=[any_space] * 4,
            out_specs=[pl.BlockSpec(memory_space=pltpu.HBM)] * 4,
            scratch_shapes=[pltpu.SemaphoreType.DMA((16,))],
            compiler_params=pltpu.CompilerParams(vmem_limit_bytes=2**20),
            name="write_out",
        )(*results)

    tokens, columns, rows = P("dp", None), P(None, "tp"), P("tp", None)
    return jax.shard_map(
        step,
        mesh=mesh,
        in_specs=(tokens, tokens, P("dp", "tp"), P("dp", "tp"), columns, columns, rows),
        out_specs=(tokens, P("dp", "tp"), P("dp", "tp"), P(("dp", "tp"), None)),
        check_vma=False,
    )
```

time: 195 us -> 111 us (0.57)
  the two profiles are of different devices: /device:TPU:97 before, /device:TPU:96 now
where the time goes in v1:
time: 111 us
  Pallas kernels  110 us (99%)
    pallas_call x1, Pallas kernels, step(): pl.pallas_call(functools.partial(body, chunks), out_shape=[pltpu.VMEM(s,...  105 us
    pallas_call x1, Pallas kernels, step(): pl.pallas_call(write_out, out_shape=[jax.ShapeDtypeStruct(s, bf16) for s...  5.37 us

profile of v1, /device:TPU:96, one launch (start us, length us, event | category | flops | bytes accessed | tf_op | source)
XLA Modules:
  0.0 111.3 jit_solution(1912949615763419056)
XLA Ops:
  0.6 105.1 %backward.1 = (bf16[2048,2048]{1,0:T(8,128)(2,1)S(1)}, bf16[2048,512]{1,0:T(8,128)(2,1)S(1)}, bf16[2048,512]{1,0:T(8,128)(2,1)S(1)}, bf16[512,2048]{1,0:T(8,128)(2,1)S(1)}) custom-call(bf16[2048,2048]{1,0:T(8,128)(2,1)} %x.1, bf16[2048,2048]{1,0:T(8,128)(2,1)} %dy.1, bf16[2048,512]{1,0:T(8,128)(2,1)} %gate.1, bf16[2048,512]{1,0:T(8,128)(2,1)} %up.1, ...), custom_call_target="tpu_custom_call" | custom-call | flops 25769803776 | bytes 31457280 | tf_op jit(solution)/shard_map/backward/pallas_call | solution.py:421
  105.7 5.4 %write_out.1 = (bf16[2048,2048]{1,0:T(8,128)(2,1)}, bf16[2048,512]{1,0:T(8,128)(2,1)}, bf16[2048,512]{1,0:T(8,128)(2,1)}, bf16[512,2048]{1,0:T(8,128)(2,1)}) custom-call(bf16[2048,2048]{1,0:T(8,128)(2,1)S(1)} %get-tuple-element.8.refs_0_, bf16[2048,512]{1,0:T(8,128)(2,1)S(1)} %get-tuple-element.9.refs_1_, bf16[2048,512]{1,0:T(8,128)(2,1)S(1)} %get-tuple-element.10.refs_2_, ...), custom_call_target="tpu_custom_call" | custom-call | tf_op jit(solution)/shard_map/write_out/pallas_call | solution.py:450

commit v2 on v1

v2 whole, which is shorter than its diff:
```python
import functools
import math

import jax
import jax.numpy as jnp
from jax import lax
from jax.experimental import pallas as pl
from jax.experimental.pallas import tpu as pltpu
from jax.sharding import PartitionSpec as P

SIDE = 4
CHUNKS = (256, 512, 768, 512)
A, B, C, A2, B2, C2, G20, G21, R2, G10, G11, R1 = range(12)
NT = (((1,), (1,)), ((), ()))
NN = (((1,), (0,)), ((), ()))


def dot(a, b, dims):
    return lax.dot_general(a, b, dims, preferred_element_type=jnp.float32)


def chunk_rows(rows):
    return [rows * c // sum(CHUNKS) for c in CHUNKS]


def body(chunks, x, dy, gate, up, w_gate, w_up, w_down, dx, dw_gate, dw_up, dw_down,
         wd, wgu, dgu, hid_t, dyb, gub, xb, xt, st_a, st_b, r_a, r_bc, c_term, own,
         s2_a, s2_b, r2_a, r2_bc, lsem, ssem, rsem, end_sem):
    d = x.shape[1]
    ff = gate.shape[1]
    nb = d // (2 * SIDE)
    starts = [sum(chunks[:k]) for k in range(len(chunks))]
    t = lax.axis_index("tp")
    px, py = lax.div(t, SIDE), lax.rem(t, SIDE)

    def to(axis, s):
        step = 1 + (SIDE - 2) * s
        return lax.rem(px + (1 - axis) * step, SIDE) * SIDE + lax.rem(py + axis * step, SIDE)

    def on(axis):
        return px * (1 - axis) + py * axis

    def local(src, dst, i):
        return pltpu.make_async_copy(src, dst, lsem.at[i])

    def send(kind, recv, i, src, dst, axis):
        return pltpu.make_async_remote_copy(
            src_ref=src, dst_ref=dst, send_sem=ssem.at[kind], recv_sem=recv,
            device_id={"tp": to(axis, lax.rem(i, 2))}, device_id_type=pl.DeviceIdType.MESH,
        )

    def all_of(recv, ref):
        send(A, recv, 0, ref, ref, 0).wait_recv()

    def loop(n, f):
        lax.fori_loop(0, n, lambda i, c: (f(i), c)[1], 0)

    nk = len(chunks)
    wd_parts = 2
    slots = (0, max(chunks[::2]))

    def load_wd(n):
        rows = pl.ds(n * (ff // wd_parts), ff // wd_parts)
        return local(w_down.at[rows], wd.at[rows], n)

    def load_dy(k):
        rows = pl.ds(starts[k], chunks[k])
        return local(dy.at[rows], dyb.at[rows], 2 + k)

    def load_gu(k):
        rows, slot, sem = pl.ds(starts[k], chunks[k]), pl.ds(slots[k % 2], chunks[k]), 2 + nk + k
        return local(gate.at[rows], gub.at[0, slot], sem), local(up.at[rows], gub.at[1, slot], sem)

    def wait_gu(k):
        ref = gub.at[:, pl.ds(slots[k % 2], chunks[k])]
        local(ref, ref, 2 + nk + k).wait()

    def load_x(j, slot):
        return local(x.at[:, pl.ds(pl.multiple_of(j * nb, nb), nb)], xb.at[slot], 2 + 2 * nk + slot)

    def mod(v):
        return lax.rem(v, SIDE)

    def w_rows(h, n):
        return pl.ds(pl.multiple_of((h * SIDE + mod(on(h) + n)) * nb, nb), nb)

    def load_w(h, n):
        rows, sem = w_rows(h, n), 4 + 2 * nk + h * SIDE + n
        return local(w_gate.at[rows], wgu.at[rows, pl.ds(0, ff)], sem), local(w_up.at[rows], wgu.at[rows, pl.ds(ff, ff)], sem)

    def wait_w(h, n):
        ref = wgu.at[w_rows(h, n)]
        local(ref, ref, 4 + 2 * nk + h * SIDE + n).wait()

    def start(*copies):
        for c in copies:
            c.start()

    start(load_wd(0), load_dy(0), *load_gu(0), load_wd(1))

    def start_weights():
        start(*load_w(0, 2), *load_w(1, 2), *load_w(0, 1), *load_w(0, 3), *load_w(1, 1), *load_w(1, 3))

    def start_rest():
        if nk > 1:
            start(load_dy(1), *load_gu(1))
        start(*load_w(0, 0), *load_w(1, 0))
        start(*[load_dy(k) for k in range(2, nk)])
        start(load_x(0, 0), load_x(1, 1))

    barrier = pltpu.get_barrier_semaphore()
    for axis in range(2):
        for s in range(2):
            pl.semaphore_signal(barrier, inc=1, device_id={"tp": to(axis, s)}, device_id_type=pl.DeviceIdType.MESH)

    def ru(k):
        return chunks[k] // 2

    def rs(k):
        return chunks[k] // (2 * SIDE)

    def unit_rows(k, u):
        return pl.ds(starts[k] + u * ru(k), ru(k))

    def u1(k):
        return pl.ds(starts[k] // 2, ru(k))

    def u2(k):
        return pl.ds(starts[k] // (2 * SIDE), rs(k))

    def term(k, u, h, j):
        w = pl.ds(pl.multiple_of((h * SIDE + j) * nb, nb), nb)
        return dot(dgu[unit_rows(k, u), :], wgu[w, :], NT)

    def block(k, h, j):
        w = pl.ds(pl.multiple_of((h * SIDE + j) * nb, nb), nb)
        return dot(dgu[pl.ds(starts[k], chunks[k]), :], wgu[w, :], NT)

    def sub(k, q):
        return pl.ds(pl.multiple_of(starts[k] // 2 + q * rs(k), 16), rs(k))

    def region(k, u, h, j, q=None):
        cols = pl.ds(pl.multiple_of((h * SIDE + j) * nb, nb), nb)
        if q is None:
            return dx.at[pl.ds(pl.multiple_of(starts[k] + u * ru(k), 16), ru(k)), cols]
        return dx.at[pl.ds(pl.multiple_of(starts[k] + u * ru(k) + q * rs(k), 16), rs(k)), cols]

    def m_a(k, i, h):
        return send(A, rsem.at[k, h], i, st_a.at[i, u1(k)], r_a.at[i, u1(k)], h)

    def m_b(k, i, h):
        return send(B, rsem.at[k, 2 + h], i, st_b.at[i, u1(k)], r_bc.at[h, lax.rem(i, 2), u1(k)], h)

    def m_c(k, i, h):
        return send(C, rsem.at[k, 2 + h], i, r_a.at[i, u1(k)], r_bc.at[h, 2 + lax.rem(i, 2), u1(k)], h)

    def m_a2(k, i, h):
        return send(A2, rsem.at[k, 4 + h], i, s2_a.at[i, u2(k)], r2_a.at[i, u2(k)], 1 - h)

    def m_b2(k, i, h):
        return send(B2, rsem.at[k, 6 + h], i, s2_b.at[i, u2(k)], r2_bc.at[h, lax.rem(i, 2), u2(k)], 1 - h)

    def m_c2(k, i, h):
        return send(C2, rsem.at[k, 6 + h], i, r2_a.at[i, u2(k)], r2_bc.at[h, 2 + lax.rem(i, 2), u2(k)], 1 - h)

    def m_g2(k, i, h, s, n):
        where = region(k, s if n == 0 else 1 - s, h, on(h), on(1 - h))
        return send(G20 + n, rsem.at[k, (4 if n else 2) + h], i, where, where, 1 - h)

    def m_r2(k, i, h, s):
        where = region(k, s, h, on(h), mod(on(1 - h) + SIDE - 1 + 2 * s))
        return send(R2, rsem.at[k, 4 + h], i, where, where, 1 - h)

    def m_g1(k, i, h, s, n):
        where = region(k, s if n == 0 else 1 - s, h, on(h))
        return send(G10 + n, rsem.at[k, h] if n == 0 else end_sem, i, where, where, h)

    def m_r1(k, i, h, s):
        where = region(k, s, h, mod(on(h) + SIDE - 1 + 2 * s))
        return send(R1, end_sem, i, where, where, h)

    def hs(i):
        return lax.div(i, 2), lax.rem(i, 2)

    def bf(v):
        return v.astype(jnp.bfloat16)

    def f32(v):
        return v.astype(jnp.float32)

    def stage_hidden(k):
        nn = ff // wd_parts
        full = max((chunks[k] - 128) // 256, 0)
        last = chunks[k] - 256 * full
        load_dy(k).wait()
        wait_gu(k)
        if k == 0:
            start_weights()
        if k == 0 and full:
            for n in range(wd_parts):
                load_wd(n).wait()

        def tile(m, size):
            rows = pl.ds(pl.multiple_of(starts[k] + m * 256, 128), size)
            part = pl.ds(pl.multiple_of(slots[k % 2] + m * 256, 128), size)
            for n in range(wd_parts):
                cols = pl.ds(n * nn, nn)
                if k == 0 and not full:
                    load_wd(n).wait()
                dh = dot(dyb[rows, :], wd[cols, :], NT)
                g, v = f32(gub[0, part, cols]), f32(gub[1, part, cols])
                sg = 1.0 / (1.0 + jnp.exp(-g))
                silu = g * sg
                dgu[rows, cols] = bf(dh * v * (sg + silu * (1.0 - sg)))
                dgu[rows, pl.ds(ff + n * nn, nn)] = bf(dh * silu)
                hid_t[cols, rows] = bf(silu * v).T

        if full:
            loop(full, lambda m: tile(m, 256))
        tile(full, last)
        if k == 0:
            start_rest()
        if k + 2 < nk:
            for c in load_gu(k + 2):
                c.start()

    def stage_a(k):
        def half(h):
            if k == 0:
                wait_w(h, 2)
            both = bf(block(k, h, mod(on(h) + 2)))
            for s in range(2):
                st_a[2 * h + s, u1(k), :] = both[s * ru(k) : (s + 1) * ru(k)]
            if k == 0:
                pl.when(h == 0)(lambda: pl.semaphore_wait(barrier, 4))
            for s in range(2):
                m_a(k, 2 * h + s, h).start()

        loop(2, half)

    def stage_b(k):
        def each(i):
            h, s = hs(i)
            if k == 0:
                wait_w(h, 1 + 2 * s)
            j = mod(on(h) + 1 + 2 * s)
            st_b[i, u1(k), :] = bf(term(k, 1 - s, h, j))
            m_b(k, i, h).start()

        loop(4, each)

    def stage_ct(k):
        def each(i):
            h, s = hs(i)
            c_term[i, u1(k), :] = term(k, s, h, mod(on(h) + 1 + 2 * s))

        loop(4, each)

    def stage_c(k):
        def each(h):
            all_of(rsem.at[k, h], r_a.at[pl.ds(2 * h, 2), u1(k)])
            for s in range(2):
                i = 2 * h + s
                r_a[i, u1(k), :] = bf(c_term[i, u1(k), :] + f32(r_a[i, u1(k), :]))
                m_c(k, i, h).start()

        loop(2, each)

    def stage_own(k):
        def each(h):
            if k == 0:
                wait_w(h, 0)
            both = block(k, h, on(h))
            for u in range(2):
                own[h, u, u1(k), :] = both[u * ru(k) : (u + 1) * ru(k)]

        loop(2, each)

    def stage_o(k):
        def each(h):
            all_of(rsem.at[k, 2 + h], r_bc.at[h, :, u1(k)])
            for u in range(2):
                own[h, u, u1(k), :] += f32(r_bc[h, 2 + u, u1(k), :]) + f32(r_bc[h, 1 - u, u1(k), :])
            q = on(1 - h)
            for s in range(2):
                s2_a[2 * h + s, u2(k), :] = bf(own[h, s, sub(k, mod(q + 2)), :])
                m_a2(k, 2 * h + s, h).start()
            for s in range(2):
                s2_b[2 * h + s, u2(k), :] = bf(own[h, 1 - s, sub(k, mod(q + 1 + 2 * s)), :])
                m_b2(k, 2 * h + s, h).start()

        loop(2, each)

    def stage_c2(k):
        def each(h):
            all_of(rsem.at[k, 4 + h], r2_a.at[pl.ds(2 * h, 2), u2(k)])
            for s in range(2):
                i = 2 * h + s
                r2_a[i, u2(k), :] = bf(own[h, s, sub(k, mod(on(1 - h) + 1 + 2 * s)), :] + f32(r2_a[i, u2(k), :]))
                m_c2(k, i, h).start()

        loop(2, each)

    def stage_o2(k):
        def each(h):
            all_of(rsem.at[k, 6 + h], r2_bc.at[h, :, u2(k)])
            q = on(1 - h)
            for u in range(2):
                total = own[h, u, sub(k, q), :] + f32(r2_bc[h, 2 + u, u2(k), :]) + f32(r2_bc[h, 1 - u, u2(k), :])
                region(k, u, h, on(h), q)[...] = bf(total)
            for n in range(2):
                for s in range(2):
                    m_g2(k, 2 * h + s, h, s, n).start()

        loop(2, each)

    def stage_r2(k):
        def each(h):
            all_of(rsem.at[k, 2 + h], r2_a.at[pl.ds(2 * h, 2), u2(k)])
            for s in range(2):
                m_r2(k, 2 * h + s, h, s).start()

        loop(2, each)

    def stage_g1(k):
        def each(h):
            all_of(rsem.at[k, 4 + h], r2_bc.at[h, :, u2(k)])
            for n in range(2):
                for s in range(2):
                    m_g1(k, 2 * h + s, h, s, n).start()

        loop(2, each)

    def stage_r1(k):
        def each(h):
            all_of(rsem.at[k, h], r_a.at[pl.ds(2 * h, 2), u1(k)])
            for s in range(2):
                m_r1(k, 2 * h + s, h, s).start()

        loop(2, each)

    def finish():
        all_of(end_sem, r_bc)
        for kinds, ref in (((A, B, C, G10, G11, R1), st_a), ((A2, B2, C2, G20, G21, R2), s2_a)):
            for kind in kinds:
                send(kind, end_sem, 0, ref, ref, 0).wait_send()

    tiles = d // nb

    def tile_gu(j):
        slot = lax.rem(j, 2)
        load_x(j, slot).wait()
        xt[...] = xb[slot].T
        pl.when(j + 2 < tiles)(lambda: load_x(j + 2, slot).start())
        nn = min(256, ff)
        rows = pl.ds(pl.multiple_of(j * nb, nb), nb)

        def cols_of(n):
            cols = pl.ds(pl.multiple_of(n * nn, nn), nn)
            dw_gate[rows, cols] = bf(dot(xt[...], dgu[:, cols], NN))
            up_cols = pl.ds(pl.multiple_of(ff + n * nn, nn), nn)
            dw_up[rows, cols] = bf(dot(xt[...], dgu[:, up_cols], NN))

        loop(ff // nn, cols_of)

    def tile_d(j):
        cols = pl.ds(pl.multiple_of(j * nb, nb), nb)
        mm = min(256, ff)

        def rows_of(m):
            rows = pl.ds(pl.multiple_of(m * mm, mm), mm)
            dw_down[rows, cols] = bf(dot(hid_t[rows, :], dyb[:, cols], NN))

        loop(ff // mm, rows_of)

    done = [0]

    def weights(n):
        lo, hi = done[0], min(done[0] + n, 2 * tiles)
        done[0] = hi
        a, b = min(lo, tiles), min(hi, tiles)
        if b > a:
            lax.fori_loop(a, b, lambda j, c: (tile_gu(j), c)[1], 0)
        a, b = max(lo, tiles) - tiles, max(hi, tiles) - tiles
        if b > a:
            lax.fori_loop(a, b, lambda j, c: (tile_d(j), c)[1], 0)

    for name, k in order():
        if name == "w":
            weights(k)
        else:
            {"h": stage_hidden, "a": stage_a, "b": stage_b, "ct": stage_ct, "c": stage_c, "own": stage_own, "o": stage_o, "c2": stage_c2,
             "o2": stage_o2, "r2": stage_r2, "g1": stage_g1, "r1": stage_r1}[name](k)
    weights(2 * tiles)
    finish()


ORDER = (
    "h0 a0 b0 h1", "a1 b1 h2 a2", "own0 ct2 ct1 h3", "c1 ct0 ct3 c0", "own1 c2 w1 b2", "w1 o1 own2 a3", "o0 own3 c21 o2",
    "b3 w1 c20 c22", "o21 c3 o20 o22", "r21 r20 o3 r22", "g11 w1 c23 g10", "w1 g12 w1 w1", "o23 r11 w1 w1", "r10 r23 w1 w1",
    "w1 r12 g13 r13", "w1 w1 w1 w1",
)


def order():
    return [(word[:-1], int(word[-1])) for words in ORDER for word in words.split()]


def write_out(*refs):
    n = (len(refs) - 1) // 2
    sem = refs[-1]
    copies = []
    for a, o in zip(refs[:n], refs[n : 2 * n]):
        parts = 4 if a.shape[0] * a.shape[1] > 2**21 else 1
        size = a.shape[0] // parts
        for i in range(parts):
            rows = pl.ds(i * size, size)
            copies.append(pltpu.make_async_copy(a.at[rows], o.at[rows], sem.at[len(copies)]))
    for c in copies:
        c.start()
    for c in copies:
        c.wait()


def solution(mesh):
    assert mesh.shape["tp"] == SIDE * SIDE

    def step(x, dy, gate, up, w_gate, w_up, w_down):
        rows, d = x.shape
        ff = gate.shape[1]
        nb = d // (2 * SIDE)
        chunks = chunk_rows(rows)
        nk = len(chunks)
        bf16, f32 = jnp.bfloat16, jnp.float32
        any_space = pl.BlockSpec(memory_space=pl.ANY)
        vmem = pl.BlockSpec(memory_space=pltpu.VMEM)
        shapes = [(rows, d), (d, ff), (d, ff), (ff, d)]
        flops = 2 * 6 * rows * d * ff
        results = pl.pallas_call(
            functools.partial(body, chunks),
            out_shape=[pltpu.VMEM(s, bf16) for s in shapes],
            in_specs=[any_space] * 7,
            out_specs=[vmem] * 4,
            scratch_shapes=[
                pltpu.VMEM((ff, d), bf16),
                pltpu.VMEM((d, 2 * ff), bf16),
                pltpu.VMEM((rows, 2 * ff), bf16),
                pltpu.VMEM((ff, rows), bf16),
                pltpu.VMEM((rows, d), bf16),
                pltpu.VMEM((2, max(chunks[::2]) + max(chunks[1::2]), ff), bf16),
                pltpu.VMEM((2, rows, nb), bf16),
                pltpu.VMEM((nb, rows), bf16),
                *[pltpu.VMEM((4, rows // 2, nb), bf16) for _ in range(3)],
                pltpu.VMEM((2, 4, rows // 2, nb), bf16),
                pltpu.VMEM((4, rows // 2, nb), f32),
                pltpu.VMEM((2, 2, rows // 2, nb), f32),
                *[pltpu.VMEM((4, rows // (2 * SIDE), nb), bf16) for _ in range(3)],
                pltpu.VMEM((2, 4, rows // (2 * SIDE), nb), bf16),
                pltpu.SemaphoreType.DMA((4 + 2 * nk + 2 * SIDE,)),
                pltpu.SemaphoreType.DMA((12,)),
                pltpu.SemaphoreType.DMA((nk, 8)),
                pltpu.SemaphoreType.DMA,
            ],
            compiler_params=pltpu.CompilerParams(
                collective_id=0, has_side_effects=True, vmem_limit_bytes=50944 * 2**10
            ),
            cost_estimate=pl.CostEstimate(flops=flops, bytes_accessed=30 * 2**20, transcendentals=rows * ff),
            name="backward",
        )(x, dy, gate, up, w_gate, w_up, w_down)
        return pl.pallas_call(
            write_out,
            out_shape=[jax.ShapeDtypeStruct(s, bf16) for s in shapes],
            in_specs=[any_space] * 4,
            out_specs=[pl.BlockSpec(memory_space=pltpu.HBM)] * 4,
            scratch_shapes=[pltpu.SemaphoreType.DMA((16,))],
            compiler_params=pltpu.CompilerParams(vmem_limit_bytes=2**20),
            name="write_out",
        )(*results)

    tokens, columns, rows = P("dp", None), P(None, "tp"), P("tp", None)
    return jax.shard_map(
        step,
        mesh=mesh,
        in_specs=(tokens, tokens, P("dp", "tp"), P("dp", "tp"), columns, columns, rows),
        out_specs=(tokens, P("dp", "tp"), P("dp", "tp"), P(("dp", "tp"), None)),
        check_vma=False,
    )
```

time: 111 us -> 103 us (0.928)
  the two profiles are of different devices: /device:TPU:96 before, /device:TPU:97 now
where the time goes in v2:
time: 103 us
  Pallas kernels  103 us (100%)
    pallas_call x1, Pallas kernels, step(): pl.pallas_call(functools.partial(body, chunks), out_shape=[pltpu.VMEM(s,...  97.2 us
    pallas_call x1, Pallas kernels, step(): pl.pallas_call(write_out, out_shape=[jax.ShapeDtypeStruct(s, bf16) for s...  5.37 us

profile of v2, /device:TPU:97, one launch (start us, length us, event | category | flops | bytes accessed | tf_op | source)
XLA Modules:
  0.0 103.4 jit_solution(10691229244278126299)
XLA Ops:
  0.6 97.2 %backward.1 = (bf16[2048,2048]{1,0:T(8,128)(2,1)S(1)}, bf16[2048,512]{1,0:T(8,128)(2,1)S(1)}, bf16[2048,512]{1,0:T(8,128)(2,1)S(1)}, bf16[512,2048]{1,0:T(8,128)(2,1)S(1)}) custom-call(bf16[2048,2048]{1,0:T(8,128)(2,1)} %x.1, bf16[2048,2048]{1,0:T(8,128)(2,1)} %dy.1, bf16[2048,512]{1,0:T(8,128)(2,1)} %gate.1, bf16[2048,512]{1,0:T(8,128)(2,1)} %up.1, ...), custom_call_target="tpu_custom_call" | custom-call | flops 25769803776 | bytes 31457280 | tf_op jit(solution)/shard_map/backward/pallas_call | solution.py:439
  97.8 5.4 %write_out.1 = (bf16[2048,2048]{1,0:T(8,128)(2,1)}, bf16[2048,512]{1,0:T(8,128)(2,1)}, bf16[2048,512]{1,0:T(8,128)(2,1)}, bf16[512,2048]{1,0:T(8,128)(2,1)}) custom-call(bf16[2048,2048]{1,0:T(8,128)(2,1)S(1)} %get-tuple-element.8.refs_0_, bf16[2048,512]{1,0:T(8,128)(2,1)S(1)} %get-tuple-element.9.refs_1_, bf16[2048,512]{1,0:T(8,128)(2,1)S(1)} %get-tuple-element.10.refs_2_, ...), custom_call_target="tpu_custom_call" | custom-call | tf_op jit(solution)/shard_map/write_out/pallas_call | solution.py:470

commit v3 on v2

--- a/solution.py
+++ b/solution.py
@@ -9,8 +9,8 @@
 from jax.sharding import PartitionSpec as P
 
 SIDE = 4
-CHUNKS = (256, 512, 768, 512)
-A, B, C, A2, B2, C2, G20, G21, R2, G10, G11, R1 = range(12)
+CHUNKS = (256, 384, 640, 768)
+A, B, C, AB2, C2, G20, G21, R2, G10, G11, R1 = range(11)
 NT = (((1,), (1,)), ((), ()))
 NN = (((1,), (0,)), ((), ()))
 
@@ -25,7 +25,7 @@
 
 def body(chunks, x, dy, gate, up, w_gate, w_up, w_down, dx, dw_gate, dw_up, dw_down,
          wd, wgu, dgu, hid_t, dyb, gub, xb, xt, st_a, st_b, r_a, r_bc, c_term, own,
-         s2_a, s2_b, r2_a, r2_bc, lsem, ssem, rsem, end_sem):
+         s2_ab, r2_ab, r2_c, lsem, ssem, rsem, end_sem):
     d = x.shape[1]
     ff = gate.shape[1]
     nb = d // (2 * SIDE)
@@ -154,14 +154,11 @@
     def m_c(k, i, h):
         return send(C, rsem.at[k, 2 + h], i, r_a.at[i, u1(k)], r_bc.at[h, 2 + lax.rem(i, 2), u1(k)], h)
 
-    def m_a2(k, i, h):
-        return send(A2, rsem.at[k, 4 + h], i, s2_a.at[i, u2(k)], r2_a.at[i, u2(k)], 1 - h)
-
-    def m_b2(k, i, h):
-        return send(B2, rsem.at[k, 6 + h], i, s2_b.at[i, u2(k)], r2_bc.at[h, lax.rem(i, 2), u2(k)], 1 - h)
+    def m_ab2(k, i, h):
+        return send(AB2, rsem.at[k, 4 + h], i, s2_ab.at[i, :, u2(k)], r2_ab.at[i, :, u2(k)], 1 - h)
 
     def m_c2(k, i, h):
-        return send(C2, rsem.at[k, 6 + h], i, r2_a.at[i, u2(k)], r2_bc.at[h, 2 + lax.rem(i, 2), u2(k)], 1 - h)
+        return send(C2, rsem.at[k, 6 + h], i, r2_ab.at[i, 0, u2(k)], r2_c.at[i, u2(k)], 1 - h)
 
     def m_g2(k, i, h, s, n):
         where = region(k, s if n == 0 else 1 - s, h, on(h), on(1 - h))
@@ -178,9 +175,6 @@
     def m_r1(k, i, h, s):
         where = region(k, s, h, mod(on(h) + SIDE - 1 + 2 * s))
         return send(R1, end_sem, i, where, where, h)
-
-    def hs(i):
-        return lax.div(i, 2), lax.rem(i, 2)
 
     def bf(v):
         return v.astype(jnp.bfloat16)
@@ -239,22 +233,22 @@
         loop(2, half)
 
     def stage_b(k):
-        def each(i):
-            h, s = hs(i)
-            if k == 0:
-                wait_w(h, 1 + 2 * s)
-            j = mod(on(h) + 1 + 2 * s)
-            st_b[i, u1(k), :] = bf(term(k, 1 - s, h, j))
-            m_b(k, i, h).start()
-
-        loop(4, each)
+        def each(h):
+            for s in range(2):
+                if k == 0:
+                    wait_w(h, 1 + 2 * s)
+                st_b[2 * h + s, u1(k), :] = bf(term(k, 1 - s, h, mod(on(h) + 1 + 2 * s)))
+            for s in range(2):
+                m_b(k, 2 * h + s, h).start()
+
+        loop(2, each)
 
     def stage_ct(k):
-        def each(i):
-            h, s = hs(i)
-            c_term[i, u1(k), :] = term(k, s, h, mod(on(h) + 1 + 2 * s))
-
-        loop(4, each)
+        def each(h):
+            for s in range(2):
+                c_term[2 * h + s, u1(k), :] = term(k, s, h, mod(on(h) + 1 + 2 * s))
+
+        loop(2, each)
 
     def stage_c(k):
         def each(h):
@@ -283,30 +277,29 @@
                 own[h, u, u1(k), :] += f32(r_bc[h, 2 + u, u1(k), :]) + f32(r_bc[h, 1 - u, u1(k), :])
             q = on(1 - h)
             for s in range(2):
-                s2_a[2 * h + s, u2(k), :] = bf(own[h, s, sub(k, mod(q + 2)), :])
-                m_a2(k, 2 * h + s, h).start()
-            for s in range(2):
-                s2_b[2 * h + s, u2(k), :] = bf(own[h, 1 - s, sub(k, mod(q + 1 + 2 * s)), :])
-                m_b2(k, 2 * h + s, h).start()
+                s2_ab[2 * h + s, 0, u2(k), :] = bf(own[h, s, sub(k, mod(q + 2)), :])
+                s2_ab[2 * h + s, 1, u2(k), :] = bf(own[h, 1 - s, sub(k, mod(q + 1 + 2 * s)), :])
+            for s in range(2):
+                m_ab2(k, 2 * h + s, h).start()
 
         loop(2, each)
 
     def stage_c2(k):
         def each(h):
-            all_of(rsem.at[k, 4 + h], r2_a.at[pl.ds(2 * h, 2), u2(k)])
+            all_of(rsem.at[k, 4 + h], r2_ab.at[pl.ds(2 * h, 2), :, u2(k)])
             for s in range(2):
                 i = 2 * h + s
-                r2_a[i, u2(k), :] = bf(own[h, s, sub(k, mod(on(1 - h) + 1 + 2 * s)), :] + f32(r2_a[i, u2(k), :]))
+                r2_ab[i, 0, u2(k), :] = bf(own[h, s, sub(k, mod(on(1 - h) + 1 + 2 * s)), :] + f32(r2_ab[i, 0, u2(k), :]))
                 m_c2(k, i, h).start()
 
         loop(2, each)
 
     def stage_o2(k):
         def each(h):
-            all_of(rsem.at[k, 6 + h], r2_bc.at[h, :, u2(k)])
+            all_of(rsem.at[k, 6 + h], r2_c.at[pl.ds(2 * h, 2), u2(k)])
             q = on(1 - h)
             for u in range(2):
-                total = own[h, u, sub(k, q), :] + f32(r2_bc[h, 2 + u, u2(k), :]) + f32(r2_bc[h, 1 - u, u2(k), :])
+                total = own[h, u, sub(k, q), :] + f32(r2_c[2 * h + u, u2(k), :]) + f32(r2_ab[2 * h + 1 - u, 1, u2(k), :])
                 region(k, u, h, on(h), q)[...] = bf(total)
             for n in range(2):
                 for s in range(2):
@@ -316,7 +309,7 @@
 
     def stage_r2(k):
         def each(h):
-            all_of(rsem.at[k, 2 + h], r2_a.at[pl.ds(2 * h, 2), u2(k)])
+            all_of(rsem.at[k, 2 + h], r2_c.at[pl.ds(2 * h, 2), u2(k)])
             for s in range(2):
                 m_r2(k, 2 * h + s, h, s).start()
 
@@ -324,7 +317,7 @@
 
     def stage_g1(k):
         def each(h):
-            all_of(rsem.at[k, 4 + h], r2_bc.at[h, :, u2(k)])
+            all_of(rsem.at[k, 4 + h], r2_ab.at[pl.ds(2 * h, 2), :, u2(k)])
             for n in range(2):
                 for s in range(2):
                     m_g1(k, 2 * h + s, h, s, n).start()
@@ -341,7 +334,7 @@
 
     def finish():
         all_of(end_sem, r_bc)
-        for kinds, ref in (((A, B, C, G10, G11, R1), st_a), ((A2, B2, C2, G20, G21, R2), s2_a)):
+        for kinds, ref in (((A, B, C, G10, G11, R1), st_a), ((C2, G20, G21, R2), r2_c), ((AB2,), s2_ab)):
             for kind in kinds:
                 send(kind, end_sem, 0, ref, ref, 0).wait_send()
 
@@ -396,9 +389,9 @@
 
 
 ORDER = (
-    "h0 a0 b0 h1", "a1 b1 h2 a2", "own0 ct2 ct1 h3", "c1 ct0 ct3 c0", "own1 c2 w1 b2", "w1 o1 own2 a3", "o0 own3 c21 o2",
-    "b3 w1 c20 c22", "o21 c3 o20 o22", "r21 r20 o3 r22", "g11 w1 c23 g10", "w1 g12 w1 w1", "o23 r11 w1 w1", "r10 r23 w1 w1",
-    "w1 r12 g13 r13", "w1 w1 w1 w1",
+    "h0 a0 b0 h1", "a1 b1 ct0 c0", "h2 a2 h3 own0", "o0 a3 b3 ct2", "ct1 c20 w1 w1", "c1 ct3 own1 own2", "c2 o20 w1 o1",
+    "b2 r20 own3 c21", "c3 o2 o21 g10", "w1 w1 w1 c22", "o3 w1 r21 r10", "w1 o22 w1 c23", "g11 w1 r22 w1", "o23 r11 r23 g12",
+    "w1 w1 g13 w1", "w1 w1 r12 r13",
 )
 
 
@@ -454,10 +447,10 @@
                 pltpu.VMEM((2, 4, rows // 2, nb), bf16),
                 pltpu.VMEM((4, rows // 2, nb), f32),
                 pltpu.VMEM((2, 2, rows // 2, nb), f32),
-                *[pltpu.VMEM((4, rows // (2 * SIDE), nb), bf16) for _ in range(3)],
-                pltpu.VMEM((2, 4, rows // (2 * SIDE), nb), bf16),
+                *[pltpu.VMEM((4, 2, rows // (2 * SIDE), nb), bf16) for _ in range(2)],
+                pltpu.VMEM((4, rows // (2 * SIDE), nb), bf16),
                 pltpu.SemaphoreType.DMA((4 + 2 * nk + 2 * SIDE,)),
-                pltpu.SemaphoreType.DMA((12,)),
+                pltpu.SemaphoreType.DMA((11,)),
                 pltpu.SemaphoreType.DMA((nk, 8)),
                 pltpu.SemaphoreType.DMA,
             ],

time: 103 us -> 102 us (level)
  Pallas kernels: 103 us -> 101 us
    pallas_call x1, Pallas kernels: 97.2 us -> 96.1 us  [step(): pl.pallas_call(functools.partial(body, chunks), out_shape=[pltpu.VMEM(s,...]
where the time goes in v3:
time: 102 us
  Pallas kernels  101 us (99%)
    pallas_call x1, Pallas kernels, step(): pl.pallas_call(functools.partial(body, chunks), out_shape=[pltpu.VMEM(s,...  96.1 us
    pallas_call x1, Pallas kernels, step(): pl.pallas_call(write_out, out_shape=[jax.ShapeDtypeStruct(s, bf16) for s...  5.37 us

profile of v3, /device:TPU:97, one launch (start us, length us, event | category | flops | bytes accessed | tf_op | source)
XLA Modules:
  0.0 102.2 jit_solution(17038468050743590428)
XLA Ops:
  0.6 96.1 %backward.1 = (bf16[2048,2048]{1,0:T(8,128)(2,1)S(1)}, bf16[2048,512]{1,0:T(8,128)(2,1)S(1)}, bf16[2048,512]{1,0:T(8,128)(2,1)S(1)}, bf16[512,2048]{1,0:T(8,128)(2,1)S(1)}) custom-call(bf16[2048,2048]{1,0:T(8,128)(2,1)} %x.1, bf16[2048,2048]{1,0:T(8,128)(2,1)} %dy.1, bf16[2048,512]{1,0:T(8,128)(2,1)} %gate.1, bf16[2048,512]{1,0:T(8,128)(2,1)} %up.1, ...), custom_call_target="tpu_custom_call" | custom-call | flops 25769803776 | bytes 31457280 | tf_op jit(solution)/shard_map/backward/pallas_call | solution.py:432
  96.7 5.4 %write_out.1 = (bf16[2048,2048]{1,0:T(8,128)(2,1)}, bf16[2048,512]{1,0:T(8,128)(2,1)}, bf16[2048,512]{1,0:T(8,128)(2,1)}, bf16[512,2048]{1,0:T(8,128)(2,1)}) custom-call(bf16[2048,2048]{1,0:T(8,128)(2,1)S(1)} %get-tuple-element.8.refs_0_, bf16[2048,512]{1,0:T(8,128)(2,1)S(1)} %get-tuple-element.9.refs_1_, bf16[2048,512]{1,0:T(8,128)(2,1)S(1)} %get-tuple-element.10.refs_2_, ...), custom_call_target="tpu_custom_call" | custom-call | tf_op jit(solution)/shard_map/write_out/pallas_call | solution.py:463

commit v4 on v3

--- a/solution.py
+++ b/solution.py
@@ -65,18 +65,18 @@
 
     def load_dy(k):
         rows = pl.ds(starts[k], chunks[k])
-        return local(dy.at[rows], dyb.at[rows], 2 + k)
+        return local(dy.at[rows], dyb.at[rows], 2 + (k if k < 2 else 0 if k == 2 else k - 1))
 
     def load_gu(k):
-        rows, slot, sem = pl.ds(starts[k], chunks[k]), pl.ds(slots[k % 2], chunks[k]), 2 + nk + k
+        rows, slot, sem = pl.ds(starts[k], chunks[k]), pl.ds(slots[k % 2], chunks[k]), 1 + nk + k % 2
         return local(gate.at[rows], gub.at[0, slot], sem), local(up.at[rows], gub.at[1, slot], sem)
 
     def wait_gu(k):
         ref = gub.at[:, pl.ds(slots[k % 2], chunks[k])]
-        local(ref, ref, 2 + nk + k).wait()
+        local(ref, ref, 1 + nk + k % 2).wait()
 
     def load_x(j, slot):
-        return local(x.at[:, pl.ds(pl.multiple_of(j * nb, nb), nb)], xb.at[slot], 2 + 2 * nk + slot)
+        return local(x.at[:, pl.ds(pl.multiple_of(j * nb, nb), nb)], xb.at[slot], slot)
 
     def mod(v):
         return lax.rem(v, SIDE)
@@ -85,12 +85,12 @@
         return pl.ds(pl.multiple_of((h * SIDE + mod(on(h) + n)) * nb, nb), nb)
 
     def load_w(h, n):
-        rows, sem = w_rows(h, n), 4 + 2 * nk + h * SIDE + n
+        rows, sem = w_rows(h, n), 3 + nk + h * SIDE + n
         return local(w_gate.at[rows], wgu.at[rows, pl.ds(0, ff)], sem), local(w_up.at[rows], wgu.at[rows, pl.ds(ff, ff)], sem)
 
     def wait_w(h, n):
         ref = wgu.at[w_rows(h, n)]
-        local(ref, ref, 4 + 2 * nk + h * SIDE + n).wait()
+        local(ref, ref, 3 + nk + h * SIDE + n).wait()
 
     def start(*copies):
         for c in copies:
@@ -404,7 +404,7 @@
     sem = refs[-1]
     copies = []
     for a, o in zip(refs[:n], refs[n : 2 * n]):
-        parts = 4 if a.shape[0] * a.shape[1] > 2**21 else 1
+        parts = 2 if a.shape[0] * a.shape[1] > 2**21 else 1
         size = a.shape[0] // parts
         for i in range(parts):
             rows = pl.ds(i * size, size)
@@ -449,7 +449,7 @@
                 pltpu.VMEM((2, 2, rows // 2, nb), f32),
                 *[pltpu.VMEM((4, 2, rows // (2 * SIDE), nb), bf16) for _ in range(2)],
                 pltpu.VMEM((4, rows // (2 * SIDE), nb), bf16),
-                pltpu.SemaphoreType.DMA((4 + 2 * nk + 2 * SIDE,)),
+                pltpu.SemaphoreType.DMA((3 + nk + 2 * SIDE,)),
                 pltpu.SemaphoreType.DMA((11,)),
                 pltpu.SemaphoreType.DMA((nk, 8)),
                 pltpu.SemaphoreType.DMA,
@@ -465,7 +465,7 @@
             out_shape=[jax.ShapeDtypeStruct(s, bf16) for s in shapes],
             in_specs=[any_space] * 4,
             out_specs=[pl.BlockSpec(memory_space=pltpu.HBM)] * 4,
-            scratch_shapes=[pltpu.SemaphoreType.DMA((16,))],
+            scratch_shapes=[pltpu.SemaphoreType.DMA((5,))],
             compiler_params=pltpu.CompilerParams(vmem_limit_bytes=2**20),
             name="write_out",
         )(*results)

time: 102 us -> 102 us (level)
  no operation moved by 1% of the time
where the time goes in v4:
time: 102 us
  Pallas kernels  101 us (99%)
    pallas_call x1, Pallas kernels, step(): pl.pallas_call(functools.partial(body, chunks), out_shape=[pltpu.VMEM(s,...  96 us
    pallas_call x1, Pallas kernels, step(): pl.pallas_call(write_out, out_shape=[jax.ShapeDtypeStruct(s, bf16) for s...  5.27 us

profile of v4, /device:TPU:97, one launch (start us, length us, event | category | flops | bytes accessed | tf_op | source)
XLA Modules:
  0.0 102.1 jit_solution(16280964508963837779)
XLA Ops:
  0.6 96.0 %backward.1 = (bf16[2048,2048]{1,0:T(8,128)(2,1)S(1)}, bf16[2048,512]{1,0:T(8,128)(2,1)S(1)}, bf16[2048,512]{1,0:T(8,128)(2,1)S(1)}, bf16[512,2048]{1,0:T(8,128)(2,1)S(1)}) custom-call(bf16[2048,2048]{1,0:T(8,128)(2,1)} %x.1, bf16[2048,2048]{1,0:T(8,128)(2,1)} %dy.1, bf16[2048,512]{1,0:T(8,128)(2,1)} %gate.1, bf16[2048,512]{1,0:T(8,128)(2,1)} %up.1, ...), custom_call_target="tpu_custom_call" | custom-call | flops 25769803776 | bytes 31457280 | tf_op jit(solution)/shard_map/backward/pallas_call | solution.py:432
  96.7 5.3 %write_out.1 = (bf16[2048,2048]{1,0:T(8,128)(2,1)}, bf16[2048,512]{1,0:T(8,128)(2,1)}, bf16[2048,512]{1,0:T(8,128)(2,1)}, bf16[512,2048]{1,0:T(8,128)(2,1)}) custom-call(bf16[2048,2048]{1,0:T(8,128)(2,1)S(1)} %get-tuple-element.8.refs_0_, bf16[2048,512]{1,0:T(8,128)(2,1)S(1)} %get-tuple-element.9.refs_1_, bf16[2048,512]{1,0:T(8,128)(2,1)S(1)} %get-tuple-element.10.refs_2_, ...), custom_call_target="tpu_custom_call" | custom-call | tf_op jit(solution)/shard_map/write_out/pallas_call | solution.py:463
